TPU v7x, 16 devices: a 4x2x1 block of a 4x4x8 slice. The times are simulated.
16 devices in a mesh: dp: 4 (over y, z, core), tp: 4 (over x).
Axes of the slice: x: 4, y: 2, z: 1, core: 2. Of those that a mesh axis runs over, the one named last changes fastest.
The devices are a block of a 4x4x8 slice.
Arguments:
- x: bfloat16 [8192, 2048], P('dp'), parts along dimension 0
- dy: bfloat16 [8192, 2048], P('dp'), parts along dimension 0
- gate: bfloat16 [8192, 5632], P('dp', 'tp'), parts along dimension 0
- up: bfloat16 [8192, 5632], P('dp', 'tp'), parts along dimension 0
- w_gate: bfloat16 [2048, 5632], P(None, 'tp')
- w_up: bfloat16 [2048, 5632], P(None, 'tp')
- w_down: bfloat16 [5632, 2048], P('tp')
Outputs:
- output 1: bfloat16 [8192, 2048], P('dp'), parts along dimension 0
- output 2: bfloat16 [8192, 5632], P('dp', 'tp'), parts along dimension 0
- output 3: bfloat16 [8192, 5632], P('dp', 'tp'), parts along dimension 0
- output 4: bfloat16 [22528, 2048], P(('dp', 'tp')), parts along dimension 0
There are 4 independent parts. A program takes and returns all parts, laid end to end along the dimension named above; an argument that names none is the same for every part.
All inputs are finite; a program needn't handle non-finite values.
Results may differ from a plain program's by a relative error of at most 0.012.
Values are sent between devices in bfloat16 or wider.
A program may use at most 768 MiB of HBM per device.

v0:
```python
import functools

import jax
import jax.numpy as jnp
from jax import lax
from jax.experimental import pallas as pl
from jax.experimental.pallas import tpu as pltpu
from jax.sharding import PartitionSpec as P

F32, BF16 = jnp.float32, jnp.bfloat16
MIB = 2**20
ANY = pl.BlockSpec(memory_space=pl.ANY)
NT = (((1,), (1,)), ((), ()))
NN = (((1,), (0,)), ((), ()))
TN = (((0,), (0,)), ((), ()))
PARTS = 2
SUB = 4
TILE = 256


def dot(a, b, dims):
    return lax.dot_general(a, b, dims, preferred_element_type=F32)


def ring_kernel(n, x, dy, gate, up, w_gate, w_up, w_down,
                dx, last_0, last_1, hidden_t, dw_gate, dw_up,
                wd_v, wc_v, dy_v, g_v, u_v, h_v, dc_v, buf, ag, x_v, xt_v, dw_v,
                wd_sem, wc_sem, in_sem, h_sem, send_sem, recv_sem, gsend_sem, grecv_sem, keep_sem, last_sem,
                x_sem, dw_sem):
    me = lax.axis_index("tp")
    piece, width, ff = buf.shape[4], buf.shape[5], g_v.shape[-1]
    half = PARTS * piece
    chunks, messages, tiles = n * PARTS, PARTS * SUB, x.shape[1] // TILE

    def block_row(block, d, h):
        return pl.multiple_of((2 * lax.rem(block + 2 * n, n) + d) * half + h * piece, piece)

    def row_of(k, d):
        return block_row(me + (2 * d - 1) * (k // PARTS + 1), d, lax.rem(k, PARTS))

    def load(k):
        slot = lax.rem(k, 2)
        return [
            pltpu.make_async_copy(src.at[pl.ds(row_of(k, d), piece)], dst.at[slot, pl.ds(d * piece, piece)], in_sem.at[i, d, slot])
            for d in range(2)
            for i, (src, dst) in enumerate(((dy, dy_v), (gate, g_v), (up, u_v)))
        ]

    def save(k):
        slot = lax.rem(k, 2)
        return [
            pltpu.make_async_copy(h_v.at[slot, :, pl.ds(d * piece, piece)], hidden_t.at[:, pl.ds(row_of(k, d), piece)], h_sem.at[d, slot])
            for d in range(2)
        ]

    def down(f):
        rows = pl.ds(f, min(TILE, ff - f))
        return pltpu.make_async_copy(w_down.at[rows], wd_v.at[rows], wd_sem.at[f // TILE])

    def weight(c):
        rows = pl.ds(pl.multiple_of(c * width, width), width)
        return [
            pltpu.make_async_copy(w_gate.at[rows], wc_v.at[rows, pl.ds(0, ff)], wc_sem.at[0, c]),
            pltpu.make_async_copy(w_up.at[rows], wc_v.at[rows, pl.ds(ff, ff)], wc_sem.at[1, c]),
        ]

    def to(d):
        return {"device_id": {"tp": lax.rem(me + 1 - 2 * d + n, n)}, "device_id_type": pl.DeviceIdType.MESH}

    def hop(s, h, c, d):
        return pltpu.make_async_remote_copy(
            src_ref=buf.at[s, h, c, d], dst_ref=buf.at[s + 1, h, c, d],
            send_sem=send_sem.at[s, h, c, d], recv_sem=recv_sem.at[s, h, c, d], **to(d),
        )

    def spread(r, h, c, d):
        return pltpu.make_async_remote_copy(
            src_ref=buf.at[n - 1, h, c, d] if r == 0 else ag.at[r - 1, h, c, d], dst_ref=ag.at[r, h, c, d],
            send_sem=gsend_sem.at[r, h, c, d], recv_sem=grecv_sem.at[r, h, c, d], **to(d),
        )

    def keep(r, h, c, d):
        cols = pl.ds(pl.multiple_of(c * width, width), width)
        return pltpu.make_async_copy(
            buf.at[n - 1, h, c, d] if r == 0 else ag.at[r - 1, h, c, d],
            dx.at[pl.ds(block_row(me + (2 * d - 1) * r, d, h), piece), cols], keep_sem.at[r, h, c, d],
        )

    def hand(h, c, d):
        cols = pl.ds(pl.multiple_of(c * width, width), width)
        return pltpu.make_async_copy(
            ag.at[n - 3, h, c, d], (last_0, last_1)[d].at[pl.ds(pl.multiple_of(h * piece, piece), piece), cols], last_sem.at[h, c, d]
        )

    def load_x(j):
        cols = pl.ds(pl.multiple_of(j * TILE, TILE), TILE)
        slot = lax.rem(j, 2)
        return pltpu.make_async_copy(x.at[:, cols], x_v.at[slot], x_sem.at[slot])

    def save_dw(j):
        rows = pl.ds(pl.multiple_of(j * TILE, TILE), TILE)
        slot = lax.rem(j, 2)
        return [
            pltpu.make_async_copy(dw_v.at[slot, :, pl.ds(0, ff)], dw_gate.at[rows], dw_sem.at[0, slot]),
            pltpu.make_async_copy(dw_v.at[slot, :, pl.ds(ff, ff)], dw_up.at[rows], dw_sem.at[1, slot]),
        ]

    def start(copies):
        for copy in copies:
            copy.start()

    def wait(copies):
        for copy in copies:
            copy.wait()

    f_tiles = range(0, ff, TILE)
    now = load(0)
    start(now[::3])
    start([down(f) for f in f_tiles])
    start(now[1:3] + now[4:] + weight(0))

    barrier = pltpu.get_barrier_semaphore()
    for d in range(2):
        pl.semaphore_signal(barrier, inc=1, **to(d))
    buf[0] = jnp.zeros(buf.shape[1:], BF16)
    pl.semaphore_wait(barrier, 2)

    def grads(k, first=False):
        slot = lax.rem(k, 2)
        wait(load(k))
        if not first:
            @pl.when(k >= 2)
            def _():
                wait(save(k - 2))

        for f in f_tiles:
            size = min(TILE, ff - f)
            cols = pl.ds(f, size)
            if first:
                down(f).wait()
            dh = dot(dy_v[slot], wd_v[cols, :], NT)
            g, u = g_v[slot, :, cols].astype(F32), u_v[slot, :, cols].astype(F32)
            sig = jax.nn.sigmoid(g)
            silu = g * sig
            h_v[slot, cols, :] = (silu * u).astype(BF16).T
            d_gate = (dh * u * (sig * (1.0 + g * (1.0 - sig)))).astype(BF16)
            d_up = (dh * silu).astype(BF16)
            for d in range(2):
                rows = pl.ds(row_of(k, d), piece)
                dc_v[rows, cols] = d_gate[d * piece:(d + 1) * piece]
                dc_v[rows, pl.ds(ff + f, size)] = d_up[d * piece:(d + 1) * piece]
        start(save(k))

        @pl.when(k + 2 < chunks)
        def _():
            start(load(k + 2))

    def term(k, c, first=False):
        s, h = k // PARTS, lax.rem(k, PARTS)
        if first:
            wait(weight(c))

        @pl.when(s > 0)
        def _():
            for d in range(2):
                hop(s - 1, h, c, d).wait_recv()

        cols = pl.ds(pl.multiple_of(c * width, width), width)
        rows = [dc_v[pl.ds(row_of(k, d), piece), :] for d in range(2)]
        acc = dot(jnp.concatenate(rows, axis=0), wc_v[cols, :], NT)
        for d in range(2):
            own = acc[d * piece:(d + 1) * piece]
            buf[s, h, c, d] = (own + buf[s, h, c, d].astype(F32)).astype(BF16)

        @pl.when(s < n - 1)
        def _():
            for d in range(2):
                hop(s, h, c, d).start()

        @pl.when(s == n - 1)
        def _():
            for d in range(2):
                spread(0, h, c, d).start()
                keep(0, h, c, d).start()

    grads(0, first=True)
    for c in range(1, SUB):
        start(weight(c))
    start(load(1))

    def term0(c, _):
        term(0, c, first=True)
        return 0

    lax.fori_loop(0, SUB, term0, 0)

    def chunk(k, _):
        grads(k)

        def terms(c, _):
            term(k, c)
            return 0

        lax.fori_loop(0, SUB, terms, 0)
        return 0

    start([load_x(0), load_x(1)])
    lax.fori_loop(1, chunks, chunk, 0)

    def forward(r, m):
        h, c = m // SUB, lax.rem(m, SUB)
        for d in range(2):
            spread(r - 1, h, c, d).wait_recv()
            keep(r, h, c, d).start()
            if r < n - 2:
                spread(r, h, c, d).start()
            else:
                hand(h, c, d).start()

    per = -(-messages * (n - 3) // tiles)

    def tile(j, _):
        slot = lax.rem(j, 2)
        load_x(j).wait()
        xt_v[...] = x_v[slot].T

        @pl.when(j >= 2)
        def _():
            wait(save_dw(j - 2))

        for f in range(0, 2 * ff, 2 * TILE):
            cols = pl.ds(f, min(2 * TILE, 2 * ff - f))
            dw_v[slot, :, cols] = dot(xt_v[...], dc_v[:, cols], NN).astype(BF16)
        start(save_dw(j))

        @pl.when(j + 2 < tiles)
        def _():
            load_x(j + 2).start()

        for r in range(1, n - 2):
            for i in range(per):
                m = j * per + i

                @pl.when(m < messages)
                def _():
                    forward(r, m)
        return 0

    lax.fori_loop(0, tiles, tile, 0)

    def arrive(m, _):
        forward(n - 2, m)
        return 0

    lax.fori_loop(0, messages, arrive, 0)

    def drain(m, _):
        h, c = m // SUB, lax.rem(m, SUB)
        for d in range(2):
            for s in range(n - 1):
                hop(s, h, c, d).wait_send()
            for r in range(n - 2):
                spread(r, h, c, d).wait_send()
            for r in range(n - 1):
                keep(r, h, c, d).wait()
            hand(h, c, d).wait()
        return 0

    lax.fori_loop(0, messages, drain, 0)
    for k in range(chunks - 2, chunks):
        wait(save(k))
    for j in range(tiles - 2, tiles):
        wait(save_dw(j))


def ring(n, x, dy, gate, up, w_gate, w_up, w_down):
    (rows, d), ff = dy.shape, gate.shape[1]
    piece, width = rows // (2 * n * PARTS), d // SUB
    dma = pltpu.SemaphoreType.DMA
    each = (PARTS, SUB, 2)
    return pl.pallas_call(
        functools.partial(ring_kernel, n),
        out_shape=[
            jax.ShapeDtypeStruct((rows, d), BF16),
            jax.ShapeDtypeStruct((PARTS * piece, d), BF16),
            jax.ShapeDtypeStruct((PARTS * piece, d), BF16),
            jax.ShapeDtypeStruct((ff, rows), BF16),
            jax.ShapeDtypeStruct((d, ff), BF16),
            jax.ShapeDtypeStruct((d, ff), BF16),
        ],
        in_specs=[ANY] * 7,
        out_specs=[ANY] * 6,
        scratch_shapes=[
            pltpu.VMEM((ff, d), BF16),
            pltpu.VMEM((d, 2 * ff), BF16),
            pltpu.VMEM((2, 2 * piece, d), BF16),
            pltpu.VMEM((2, 2 * piece, ff), BF16),
            pltpu.VMEM((2, 2 * piece, ff), BF16),
            pltpu.VMEM((2, ff, 2 * piece), BF16),
            pltpu.VMEM((rows, 2 * ff), BF16),
            pltpu.VMEM((n, *each, piece, width), BF16),
            pltpu.VMEM((n - 2, *each, piece, width), BF16),
            pltpu.VMEM((2, rows, TILE), BF16),
            pltpu.VMEM((TILE, rows), BF16),
            pltpu.VMEM((2, TILE, 2 * ff), BF16),
            dma((-(-ff // TILE),)),
            dma((2, SUB)),
            dma((3, 2, 2)),
            dma((2, 2)),
            dma((n - 1, *each)),
            dma((n - 1, *each)),
            dma((n - 2, *each)),
            dma((n - 2, *each)),
            dma((n - 1, *each)),
            dma(each),
            dma((2,)),
            dma((2, 2)),
        ],
        compiler_params=pltpu.CompilerParams(
            collective_id=0, has_side_effects=True, vmem_limit_bytes=62 * MIB
        ),
        cost_estimate=pl.CostEstimate(flops=10 * rows * d * ff, bytes_accessed=16 * rows * d, transcendentals=2 * rows * ff),
        name="ring",
    )(x, dy, gate, up, w_gate, w_up, w_down)


def finish_kernel(places, hidden_t, dy, dx_in, dw_gate_in, dw_up_in, dw_down, dx, dw_gate, dw_up):
    del places
    dx[...] = dx_in[...]
    dw_gate[...] = dw_gate_in[...]
    dw_up[...] = dw_up_in[...]
    dw_down[...] = dot(hidden_t[...], dy[...], NN).astype(BF16)


def finish(n, dx, hidden_t, dy, dw_gate, dw_up):
    (rows, d), ff = dy.shape, hidden_t.shape[0]
    half, steps = rows // (2 * n), d // TILE
    me = lax.axis_index("tp")
    step = jnp.minimum(jnp.arange(steps), 2 * n - 3)
    way = step % 2
    places = 2 * ((me + (2 * way - 1) * (step // 2) + n) % n) + way
    here = lambda j, p: (j, 0)
    place = lambda j, p: (p[j], 0)
    return pl.pallas_call(
        finish_kernel,
        out_shape=[
            jax.ShapeDtypeStruct((ff, d), BF16),
            jax.ShapeDtypeStruct((rows, d), BF16),
            jax.ShapeDtypeStruct((d, ff), BF16),
            jax.ShapeDtypeStruct((d, ff), BF16),
        ],
        grid_spec=pltpu.PrefetchScalarGridSpec(
            num_scalar_prefetch=1,
            grid=(steps,),
            in_specs=[
                pl.BlockSpec((ff, rows), lambda j, p: (0, 0), pipeline_mode=pl.Buffered(1)),
                pl.BlockSpec((rows, TILE), lambda j, p: (0, j)),
                pl.BlockSpec((half, d), place),
                pl.BlockSpec((TILE, ff), here),
                pl.BlockSpec((TILE, ff), here),
            ],
            out_specs=[
                pl.BlockSpec((ff, TILE), lambda j, p: (0, j)),
                pl.BlockSpec((half, d), place),
                pl.BlockSpec((TILE, ff), here),
                pl.BlockSpec((TILE, ff), here),
            ],
        ),
        compiler_params=pltpu.CompilerParams(vmem_limit_bytes=62 * MIB),
        cost_estimate=pl.CostEstimate(flops=2 * rows * d * ff, bytes_accessed=12 * rows * d, transcendentals=0),
        name="finish",
    )(places, hidden_t, dy, dx, dw_gate, dw_up)


def solution(mesh):
    n = mesh.shape["tp"]

    def step(x, dy, gate, up, w_gate, w_up, w_down):
        me, half = lax.axis_index("tp"), x.shape[0] // (2 * n)
        dx, *last, hidden_t, dw_gate, dw_up = ring(n, x, dy, gate, up, w_gate, w_up, w_down)
        ends = [lax.ppermute(last[d], "tp", [(i, (i + 1 - 2 * d) % n) for i in range(n)]) for d in range(2)]
        dw_down, dx, dw_gate, dw_up = finish(n, dx, hidden_t, dy, dw_gate, dw_up)
        for d in range(2):
            block = lax.rem(me + (2 * d - 1) * (n - 1) + n, n)
            dx = lax.dynamic_update_slice(dx, ends[d], ((2 * block + d) * half, 0))
        return dx, dw_gate, dw_up, dw_down

    tokens, columns, rows = P("dp", None), P(None, "tp"), P("tp", None)
    return jax.shard_map(
        step,
        mesh=mesh,
        in_specs=(tokens, tokens, P("dp", "tp"), P("dp", "tp"), columns, columns, rows),
        out_specs=(tokens, P("dp", "tp"), P("dp", "tp"), P(("dp", "tp"), None)),
        check_vma=False,
    )
```

profile of v0, /device:TPU:112, one launch (start us, length us, event | category | flops | bytes accessed | tf_op | source)
XLA Modules:
  0.0 163.3 jit_solution(2023860150855634596)
XLA Ops:
  0.6 129.4 %ring.1 = (bf16[2048,2048]{1,0:T(8,128)(2,1)}, bf16[256,2048]{1,0:T(8,128)(2,1)}, bf16[256,2048]{1,0:T(8,128)(2,1)}, bf16[1408,2048]{1,0:T(8,128)(2,1)}, bf16[20...) custom-call(bf16[2048,2048]{1,0:T(8,128)(2,1)} %x.1, bf16[2048,2048]{1,0:T(8,128)(2,1)} %dy.3, bf16[2048,1408]{1,0:T(8,128)(2,1)} %gate.1, ...), custom_call_target="tpu_custom_call" | custom-call | flops 59055800320 | bytes 67108864 | tf_op jit(solution)/shard_map/ring/pallas_call | solution.py:281
  130.0 0.1 collective-permute-start
  130.1 3.2 %collective-permute-start.1 = (bf16[256,2048]{1,0:T(8,128)(2,1)}, bf16[256,2048]{1,0:T(8,128)(2,1)S(1)}, u32[]{:S(2)}, u32[]{:S(2)}) collective-permute-start(bf16[256,2048]{1,0:T(8,128)(2,1)} %get-tuple-element.20), channel_id=1, source_target_pairs={{0,3},{1,0},{2,1},{3,2},{4,7},{5,4},{6,5},{7,6},{8,11},{9,8},{10,9... | collective-permute-start | bytes 3145736 | tf_op jit(solution)/shard_map/ppermute | solution.py:381
  133.3 0.6 fusion.1.places
  133.9 26.1 %finish.1 = (bf16[1408,2048]{1,0:T(8,128)(2,1)}, bf16[2048,2048]{1,0:T(8,128)(2,1)}, bf16[2048,1408]{1,0:T(8,128)(2,1)}, bf16[2048,1408]{1,0:T(8,128)(2,1)}) custom-call(s32[8]{0:T(128)} %fusion.1.places, bf16[1408,2048]{1,0:T(8,128)(2,1)} %get-tuple-element.14.hidden_t, bf16[2048,2048]{1,0:T(8,128)(2,1)} %dy.3, bf16[2048,2048]{1,0:T(8,128)(2,1)} %get-tuple-element.15.dx_in, ...), custom_call_target="tpu_custom_call" | custom-call | flops 11811160064 | bytes 50331648 | tf_op jit(solution)/shard_map/finish/pallas_call | solution.py:344
  159.9 0.0 collective-permute-done
  160.0 2.3 %constant_dynamic-update-slice_fusion.1 = bf16[2048,2048]{1,0:T(8,128)(2,1)} fusion(bf16[2048,2048]{1,0:T(8,128)(2,1)} %get-tuple-element.18, bf16[256,2048]{1,0:T(8,128)(2,1)} %collective-permute-done, s32[]{:T(128)S(6)} %select_n.27), kind=kLoop, calls=%fused_computation.9 | loop fusion | bytes 2097156 | tf_op jit(solution)/shard_map/dynamic_update_slice | solution.py:385
  162.3 0.0 collective-permute-done.1
  162.3 1.1 constant_dynamic-update-slice_fusion
Async XLA Ops:
  130.0 29.9 %collective-permute-start = (bf16[256,2048]{1,0:T(8,128)(2,1)}, bf16[256,2048]{1,0:T(8,128)(2,1)}, u32[]{:S(2)}, u32[]{:S(2)}) collective-permute-start(bf16[256,2048]{1,0:T(8,128)(2,1)} %get-tuple-element.19), channel_id=1, source_target_pairs={{0,1},{1,2},{2,3},{3,0},{4,5},{5,6},{6,7},{7,4},{8,9},{9,10},{10,1... | collective-permute-start | bytes 3145736 | tf_op jit(solution)/shard_map/ppermute | solution.py:381
  130.1 32.1 %collective-permute-start.1 = (bf16[256,2048]{1,0:T(8,128)(2,1)}, bf16[256,2048]{1,0:T(8,128)(2,1)S(1)}, u32[]{:S(2)}, u32[]{:S(2)}) collective-permute-start(bf16[256,2048]{1,0:T(8,128)(2,1)} %get-tuple-element.20), channel_id=1, source_target_pairs={{0,3},{1,0},{2,1},{3,2},{4,7},{5,4},{6,5},{7,6},{8,11},{9,8},{10,9... | collective-permute-start | bytes 3145736 | tf_op jit(solution)/shard_map/ppermute | solution.py:381
where the time goes:
time: 164 us; the launch traced here: 163 us
  Pallas kernels  155 us (95%)
  local copies, waits for them, and re-layouts  3.39 us (2%)
  starting transfers between devices  3.31 us (2%)
    pallas_call x1, Pallas kernels, ring(): pl.pallas_call(functools.partial(ring_kernel, n), out_shape=[jax.ShapeDty...  129 us
    pallas_call x1, Pallas kernels, finish(): pl.pallas_call(finish_kernel, out_shape=[jax.ShapeDtypeStruct((ff, d), BF...  26.1 us
    dynamic_update_slice x2, local copies, waits for them, and re-layouts, step(): dx = lax.dynamic_update_slice(dx, ends[d], ((2 * block + d) * half, 0))  3.39 us
    ppermute x2, starting transfers between devices, step(): lax.ppermute(last[d], 'tp', [(i, (i + 1 - 2 * d) % n) for i in range(n)])  3.31 us
  transfers between devices with their start and end apart: 2, of which 0 were waited for; matrix products, arithmetic and copies ran while one was open for 2% of the time, Pallas kernels for 16%

commit v1 on v0

v1 whole, which is shorter than its diff:
```python
import functools

import jax
import jax.numpy as jnp
from jax import lax
from jax.experimental import pallas as pl
from jax.experimental.pallas import tpu as pltpu
from jax.sharding import PartitionSpec as P

F32, BF16 = jnp.float32, jnp.bfloat16
MIB = 2**20
ANY = pl.BlockSpec(memory_space=pl.ANY)
NT = (((1,), (1,)), ((), ()))
NN = (((1,), (0,)), ((), ()))
TN = (((0,), (0,)), ((), ()))
PARTS = 2
SUB = 4
TILE = 256


def dot(a, b, dims):
    return lax.dot_general(a, b, dims, preferred_element_type=F32)


def ring_kernel(n, x, dy, gate, up, w_gate, w_up, w_down,
                dx, last_0, last_1, dw_gate, dw_up, dw_down,
                wd_v, wc_v, dy_v, g_v, u_v, ht_v, dc_v, buf, ag, x_v, xt_v, dw_v, dd_v,
                wd_sem, wc_sem, in_sem, send_sem, recv_sem, gsend_sem, grecv_sem, end_sem, keep_sem,
                x_sem, dw_sem, dd_sem):
    me = lax.axis_index("tp")
    piece, width, ff = buf.shape[4], buf.shape[5], g_v.shape[-1]
    half = PARTS * piece
    chunks, messages, tiles = n * PARTS, PARTS * SUB, x.shape[1] // TILE

    def block_row(block, d, h):
        return pl.multiple_of((2 * lax.rem(block + 2 * n, n) + d) * half + h * piece, piece)

    def row_of(k, d):
        return block_row(me + (2 * d - 1) * (k // PARTS + 1), d, lax.rem(k, PARTS))

    def load(k):
        slot = lax.rem(k, 2)
        return [
            pltpu.make_async_copy(src.at[pl.ds(row_of(k, d), piece)], dst.at[slot, pl.ds(d * piece, piece)], in_sem.at[i, slot])
            for i, (src, dst) in enumerate(((dy, dy_v), (gate, g_v), (up, u_v)))
            for d in range(2)
        ]

    def whole(ref, sem):
        return pltpu.make_async_copy(ref, ref, sem)

    def loaded(k):
        slot = lax.rem(k, 2)
        return [whole(ref.at[slot], in_sem.at[i, slot]) for i, ref in enumerate((dy_v, g_v, u_v))]

    def down(f):
        rows = pl.ds(f, min(TILE, ff - f))
        return pltpu.make_async_copy(w_down.at[rows], wd_v.at[rows], wd_sem.at[f // TILE])

    def weight(c):
        rows = pl.ds(pl.multiple_of(c * width, width), width)
        return [
            pltpu.make_async_copy(w_gate.at[rows], wc_v.at[rows, pl.ds(0, ff)], wc_sem.at[c]),
            pltpu.make_async_copy(w_up.at[rows], wc_v.at[rows, pl.ds(ff, ff)], wc_sem.at[c]),
        ]

    def weighted(c):
        return whole(wc_v.at[pl.ds(pl.multiple_of(c * width, width), width)], wc_sem.at[c])

    def to(d):
        return {"device_id": {"tp": lax.rem(me + 1 - 2 * d + n, n)}, "device_id_type": pl.DeviceIdType.MESH}

    def hop(s, h, c, d):
        return pltpu.make_async_remote_copy(
            src_ref=buf.at[s, h, c, d], dst_ref=buf.at[s + 1, h, c, d],
            send_sem=send_sem.at[s], recv_sem=recv_sem.at[s, h, c], **to(d),
        )

    def end(h, c, d):
        cols = pl.ds(pl.multiple_of(c * width, width), width)
        return (last_0, last_1)[d].at[pl.ds(pl.multiple_of(h * piece, piece), piece), cols]

    def spread(r, h, c, d):
        return pltpu.make_async_remote_copy(
            src_ref=buf.at[n - 1, h, c, d] if r == 0 else ag.at[r - 1, h, c, d],
            dst_ref=ag.at[r, h, c, d] if r < n - 3 else end(h, c, d),
            send_sem=gsend_sem.at[r], recv_sem=grecv_sem.at[r, h, c] if r < n - 3 else end_sem.at[d], **to(d),
        )

    def keep(r, h, c, d):
        cols = pl.ds(pl.multiple_of(c * width, width), width)
        return pltpu.make_async_copy(
            buf.at[n - 1, h, c, d] if r == 0 else ag.at[r - 1, h, c, d],
            dx.at[pl.ds(block_row(me + (2 * d - 1) * r, d, h), piece), cols], keep_sem.at[r],
        )

    def load_cols(src, j):
        cols = pl.ds(pl.multiple_of(j * TILE, TILE), TILE)
        slot = lax.rem(j, 2)
        return pltpu.make_async_copy(src.at[:, cols], x_v.at[slot], x_sem.at[slot])

    def save_dd(j):
        cols = pl.ds(pl.multiple_of(j * TILE, TILE), TILE)
        slot = lax.rem(j, 2)
        return pltpu.make_async_copy(dd_v.at[slot], dw_down.at[:, cols], dd_sem.at[slot])

    def save_dw(j):
        rows = pl.ds(pl.multiple_of(j * TILE, TILE), TILE)
        slot = lax.rem(j, 2)
        return [
            pltpu.make_async_copy(dw_v.at[slot, :, pl.ds(0, ff)], dw_gate.at[rows], dw_sem.at[slot]),
            pltpu.make_async_copy(dw_v.at[slot, :, pl.ds(ff, ff)], dw_up.at[rows], dw_sem.at[slot]),
        ]

    def saved_dw(j):
        slot = lax.rem(j, 2)
        return whole(dw_v.at[slot], dw_sem.at[slot])

    def start(copies):
        for copy in copies:
            copy.start()

    def wait(copies):
        for copy in copies:
            copy.wait()

    f_tiles = range(0, ff, TILE)
    now, downs = load(0), [down(f) for f in f_tiles]
    start(now[:2] + downs[:3] + now[2:] + downs[3:])

    barrier = pltpu.get_barrier_semaphore()
    for d in range(2):
        pl.semaphore_signal(barrier, inc=1, **to(d))
    buf[0] = jnp.zeros(buf.shape[1:], BF16)

    def grads(k, first=False):
        slot = lax.rem(k, 2)
        copies = loaded(k)
        wait(copies)

        def rest(f, dh):
            size = min(TILE, ff - f)
            cols = pl.ds(f, size)
            g, u = g_v[slot, :, cols].astype(F32), u_v[slot, :, cols].astype(F32)
            sig = jax.nn.sigmoid(g)
            silu = g * sig
            hidden = (silu * u).astype(BF16).T
            d_gate = (dh * u * (sig * (1.0 + g * (1.0 - sig)))).astype(BF16)
            d_up = (dh * silu).astype(BF16)
            for d in range(2):
                rows, part = pl.ds(row_of(k, d), piece), slice(d * piece, (d + 1) * piece)
                dc_v[rows, cols] = d_gate[part]
                dc_v[rows, pl.ds(ff + f, size)] = d_up[part]
                ht_v[cols, rows] = hidden[:, part]

        dh = None
        for f in f_tiles:
            if first and f == 0:
                wait(downs[:3])
                start(weight(0))
            if first and f == 3 * TILE:
                rest(f - TILE, dh)
                wait(downs[3:])
                start(weight(1))
            before, dh = dh, dot(dy_v[slot], wd_v[pl.ds(f, min(TILE, ff - f)), :], NT)
            if f and not (first and f == 3 * TILE):
                rest(f - TILE, before)
        rest(f_tiles[-1], dh)

        @pl.when(k + 2 < chunks)
        def _():
            start(load(k + 2))

    def term(k, c, first=False):
        s, h = k // PARTS, lax.rem(k, PARTS)
        if first:
            weighted(c).wait()

        @pl.when(s > 0)
        def _():
            whole(buf.at[s, h, c], recv_sem.at[s - 1, h, c]).wait()

        cols = pl.ds(pl.multiple_of(c * width, width), width)
        rows = [dc_v[pl.ds(row_of(k, d), piece), :] for d in range(2)]
        acc = dot(jnp.concatenate(rows, axis=0), wc_v[cols, :], NT)
        for d in range(2):
            own = acc[d * piece:(d + 1) * piece]
            buf[s, h, c, d] = (own + buf[s, h, c, d].astype(F32)).astype(BF16)

        @pl.when(s < n - 1)
        def _():
            for d in range(2):
                hop(s, h, c, d).start()

        @pl.when(s == n - 1)
        def _():
            for d in range(2):
                spread(0, h, c, d).start()
                keep(0, h, c, d).start()

    grads(0, first=True)
    start(weight(2) + weight(3) + load(1))
    pl.semaphore_wait(barrier, 2)

    def term0(c, _):
        term(0, c, first=True)
        return 0

    lax.fori_loop(0, SUB, term0, 0)

    def terms(k):
        def body(c, _):
            term(k, c)
            return 0

        lax.fori_loop(0, SUB, body, 0)

    def chunk(k, _):
        grads(k)

        @pl.when(k < chunks - PARTS)
        def _():
            terms(k)
        return 0

    lax.fori_loop(1, chunks, chunk, 0)
    start([load_cols(dy, 0), load_cols(dy, 1)])

    def last_term(m, _):
        term(chunks - PARTS + m // SUB, lax.rem(m, SUB))
        slot = lax.rem(m, 2)
        load_cols(dy, m).wait()

        @pl.when(m >= 2)
        def _():
            save_dd(m - 2).wait()

        dd_v[slot] = dot(ht_v[...], x_v[slot], NN).astype(BF16)
        save_dd(m).start()

        @pl.when(m + 2 < messages)
        def _():
            load_cols(dy, m + 2).start()
        return 0

    lax.fori_loop(0, messages, last_term, 0)
    start([load_cols(x, 0), load_cols(x, 1)])

    def forward(r, m):
        h, c = m // SUB, lax.rem(m, SUB)
        whole(ag.at[r - 1, h, c], grecv_sem.at[r - 1, h, c]).wait()
        for d in range(2):
            spread(r, h, c, d).start()
            keep(r, h, c, d).start()

    per = -(-messages * (n - 3) // tiles)

    def tile(j, _):
        slot = lax.rem(j, 2)
        load_cols(x, j).wait()
        xt_v[...] = x_v[slot].T

        @pl.when(j >= 2)
        def _():
            saved_dw(j - 2).wait()

        for f in range(0, 2 * ff, 2 * TILE):
            cols = pl.ds(f, min(2 * TILE, 2 * ff - f))
            dw_v[slot, :, cols] = dot(xt_v[...], dc_v[:, cols], NN).astype(BF16)
        start(save_dw(j))

        @pl.when(j + 2 < tiles)
        def _():
            load_cols(x, j + 2).start()

        for r in range(1, n - 2):
            for i in range(per):
                m = j * per + i

                @pl.when(m < messages)
                def _():
                    forward(r, m)
        return 0

    lax.fori_loop(0, tiles, tile, 0)

    for s in range(n - 1):
        whole(buf.at[s], send_sem.at[s]).wait()
    for r in range(n - 2):
        sent = buf.at[n - 1] if r == 0 else ag.at[r - 1]
        whole(sent, keep_sem.at[r]).wait()
        whole(sent, gsend_sem.at[r]).wait()
    for j in range(tiles - 2, tiles):
        save_dd(j).wait()
        saved_dw(j).wait()
    for d, ref in enumerate((last_0, last_1)):
        whole(ref, end_sem.at[d]).wait()


def ring(n, x, dy, gate, up, w_gate, w_up, w_down):
    (rows, d), ff = dy.shape, gate.shape[1]
    piece, width = rows // (2 * n * PARTS), d // SUB
    assert n == 4 and d == PARTS * SUB * TILE
    dma = pltpu.SemaphoreType.DMA
    each = (PARTS, SUB, 2)
    return pl.pallas_call(
        functools.partial(ring_kernel, n),
        out_shape=[
            jax.ShapeDtypeStruct((rows, d), BF16),
            jax.ShapeDtypeStruct((PARTS * piece, d), BF16),
            jax.ShapeDtypeStruct((PARTS * piece, d), BF16),
            jax.ShapeDtypeStruct((d, ff), BF16),
            jax.ShapeDtypeStruct((d, ff), BF16),
            jax.ShapeDtypeStruct((ff, d), BF16),
        ],
        in_specs=[ANY] * 7,
        out_specs=[ANY] * 6,
        scratch_shapes=[
            pltpu.VMEM((ff, d), BF16),
            pltpu.VMEM((d, 2 * ff), BF16),
            pltpu.VMEM((2, 2 * piece, d), BF16),
            pltpu.VMEM((2, 2 * piece, ff), BF16),
            pltpu.VMEM((2, 2 * piece, ff), BF16),
            pltpu.VMEM((ff, rows), BF16),
            pltpu.VMEM((rows, 2 * ff), BF16),
            pltpu.VMEM((n, *each, piece, width), BF16),
            pltpu.VMEM((n - 3, *each, piece, width), BF16),
            pltpu.VMEM((2, rows, TILE), BF16),
            pltpu.VMEM((TILE, rows), BF16),
            pltpu.VMEM((2, TILE, 2 * ff), BF16),
            pltpu.VMEM((2, ff, TILE), BF16),
            dma((-(-ff // TILE),)),
            dma((SUB,)),
            dma((3, 2)),
            dma((n - 1,)),
            dma((n - 1, PARTS, SUB)),
            dma((n - 2,)),
            dma((n - 3, PARTS, SUB)),
            dma((2,)),
            dma((n - 2,)),
            dma((2,)),
            dma((2,)),
            dma((2,)),
        ],
        compiler_params=pltpu.CompilerParams(
            collective_id=0, has_side_effects=True, vmem_limit_bytes=62 * MIB
        ),
        cost_estimate=pl.CostEstimate(flops=12 * rows * d * ff, bytes_accessed=16 * rows * d, transcendentals=2 * rows * ff),
        name="ring",
    )(x, dy, gate, up, w_gate, w_up, w_down)


def finish_kernel(count, places, *refs):
    del places
    j, outs = pl.program_id(0), refs[-4:]
    dx_in, last_0, last_1 = refs[:3]
    for src, dst in zip(refs[3:6], outs[1:]):
        dst[...] = src[...]
    for low, high, src in ((0, count, dx_in), (count, count + PARTS, last_0), (count + PARTS, count + 2 * PARTS, last_1)):
        @pl.when((j >= low) & (j < high))
        def _():
            outs[0][...] = src[...]


def finish(n, dx, last_0, last_1, dw_gate, dw_up, dw_down):
    (rows, d), (ff, _) = dx.shape, dw_down.shape
    piece = rows // (2 * n * PARTS)
    count = 2 * (n - 2) * PARTS
    me, i = lax.axis_index("tp"), jnp.arange(count + 2 * PARTS)
    way = i // PARTS % 2
    places = (2 * ((me + (2 * way - 1) * (i // (2 * PARTS)) + n) % n) + way) * PARTS + i % PARTS
    steps = d // 128

    def rows_in(block, most, first=0):
        return pl.BlockSpec(block, lambda j, p: (jnp.clip(j - first, 0, most - 1), 0))

    def placed(most):
        return pl.BlockSpec((piece, d), lambda j, p: (p[jnp.minimum(j, most - 1)], 0))

    weights = [rows_in((128, ff), steps), rows_in((128, ff), steps), rows_in((128, d), ff // 128)]
    return pl.pallas_call(
        functools.partial(finish_kernel, count),
        out_shape=[jax.ShapeDtypeStruct(a.shape, a.dtype) for a in (dx, dw_gate, dw_up, dw_down)],
        grid_spec=pltpu.PrefetchScalarGridSpec(
            num_scalar_prefetch=1,
            grid=(steps,),
            in_specs=[placed(count), rows_in((piece, d), PARTS, count), rows_in((piece, d), PARTS, count + PARTS), *weights],
            out_specs=[placed(count + 2 * PARTS), *weights],
        ),
        compiler_params=pltpu.CompilerParams(vmem_limit_bytes=61 * MIB),
        cost_estimate=pl.CostEstimate(flops=2 * rows * d * ff, bytes_accessed=12 * rows * d, transcendentals=0),
        name="finish",
    )(places, dx, last_0, last_1, dw_gate, dw_up, dw_down)


def place_kernel(n, _, end_0, end_1, dx, sem):
    me, half = lax.axis_index("tp"), end_0.shape[0]
    put = []
    for d, src in enumerate((end_0, end_1)):
        row = (2 * lax.rem(me + (2 * d - 1) * (n - 1) + n, n) + d) * half
        for i in range(4):
            part = half // 4
            rows = pl.ds(pl.multiple_of(row + i * part, part), part)
            put.append(pltpu.make_async_copy(src.at[pl.ds(i * part, part)], dx.at[rows], sem.at[d, i]))
    for copy in put:
        copy.start()
    for copy in put:
        copy.wait()


def place(n, dx, ends):
    vmem = pl.BlockSpec(memory_space=pltpu.VMEM)
    return pl.pallas_call(
        functools.partial(place_kernel, n),
        out_shape=jax.ShapeDtypeStruct(dx.shape, dx.dtype),
        in_specs=[ANY, vmem, vmem],
        out_specs=ANY,
        scratch_shapes=[pltpu.SemaphoreType.DMA((2, 4))],
        input_output_aliases={0: 0},
        compiler_params=pltpu.CompilerParams(vmem_limit_bytes=16 * MIB),
        name="place",
    )(dx, *ends)


def solution(mesh):
    n = mesh.shape["tp"]

    def step(x, dy, gate, up, w_gate, w_up, w_down):
        dx, *last, dw_gate, dw_up, dw_down = ring(n, x, dy, gate, up, w_gate, w_up, w_down)
        ends = [lax.ppermute(last[d], "tp", [(i, (i + 1 - 2 * d) % n) for i in range(n)]) for d in range(2)]
        dx, dw_gate, dw_up, dw_down = finish(n, dx, *last, dw_gate, dw_up, dw_down)
        return place(n, dx, ends), dw_gate, dw_up, dw_down

    tokens, columns, rows = P("dp", None), P(None, "tp"), P("tp", None)
    return jax.shard_map(
        step,
        mesh=mesh,
        in_specs=(tokens, tokens, P("dp", "tp"), P("dp", "tp"), columns, columns, rows),
        out_specs=(tokens, P("dp", "tp"), P("dp", "tp"), P(("dp", "tp"), None)),
        check_vma=False,
    )
```

time: 164 us -> 153 us (0.933)
  Pallas kernels: 155 us -> 147 us
  local copies, waits for them, and re-layouts: 3.39 us -> 0 us
    pallas_call x1, Pallas kernels: 129 us -> 124 us  [ring(): pl.pallas_call(functools.partial(ring_kernel, n), out_shape=[jax.ShapeDty...]
    dynamic_update_slice x2 -> x0, local copies, waits for them, and re-layouts: 3.39 us -> none  [step(): dx = lax.dynamic_update_slice(dx, ends[d], ((2 * block + d) * half, 0))]
    pallas_call x1 -> x2, Pallas kernels: 26.1 us -> 22.8 us  [the longest x1 21.5 us: finish(): pl.pallas_call(functools.partial(finish_kernel, count), out_shape=[jax.Sh...]
  transfers between devices with their start and end apart: 2 -> 2, of which waited for: 0 -> 1; matrix products, arithmetic and copies ran while one was open for 2% -> 0% of each run, Pallas kernels for 16% -> 14%
where the time goes in v1:
time: 153 us; the launch traced here: 152 us
  Pallas kernels  147 us (96%)
  starting transfers between devices  3.31 us (2%)
    pallas_call x1, Pallas kernels, ring(): pl.pallas_call(functools.partial(ring_kernel, n), out_shape=[jax.ShapeDty...  124 us
    pallas_call x1, Pallas kernels, finish(): pl.pallas_call(functools.partial(finish_kernel, count), out_shape=[jax.Sh...  21.5 us
    ppermute x2, starting transfers between devices, step(): lax.ppermute(last[d], 'tp', [(i, (i + 1 - 2 * d) % n) for i in range(n)])  3.31 us
  transfers between devices with their start and end apart: 2, of which 1 were waited for; matrix products, arithmetic and copies ran while one was open for 0% of the time, Pallas kernels for 14%

profile of v1, /device:TPU:112, one launch (start us, length us, event | category | flops | bytes accessed | tf_op | source)
XLA Modules:
  0.0 152.4 jit_solution(12163543880659581010)
XLA Ops:
  0.6 124.4 %ring.1 = (bf16[2048,2048]{1,0:T(8,128)(2,1)}, bf16[256,2048]{1,0:T(8,128)(2,1)}, bf16[256,2048]{1,0:T(8,128)(2,1)}, bf16[2048,1408]{1,0:T(8,128)(2,1)}, bf16[20...) custom-call(bf16[2048,2048]{1,0:T(8,128)(2,1)} %x.1, bf16[2048,2048]{1,0:T(8,128)(2,1)} %dy.1, bf16[2048,1408]{1,0:T(8,128)(2,1)} %gate.1, ...), custom_call_target="tpu_custom_call" | custom-call | flops 70866960384 | bytes 67108864 | tf_op jit(solution)/shard_map/ring/pallas_call | solution.py:306
  125.0 0.2 collective-permute-start
  125.2 3.1 %collective-permute-start.1 = (bf16[256,2048]{1,0:T(8,128)(2,1)}, bf16[256,2048]{1,0:T(8,128)(2,1)S(1)}, u32[]{:S(2)}, u32[]{:S(2)}) collective-permute-start(bf16[256,2048]{1,0:T(8,128)(2,1)} %get-tuple-element.16.refs_2_), channel_id=1, source_target_pairs={{0,3},{1,0},{2,1},{3,2},{4,7},{5,4},{6,5},{7,6},{8,11},{9,8},{10,9... | collective-permute-start | bytes 3145736 | tf_op jit(solution)/shard_map/ppermute | solution.py:430
  128.3 0.6 fusion.places
  128.9 21.5 %finish.1 = (bf16[2048,2048]{1,0:T(8,128)(2,1)}, bf16[2048,1408]{1,0:T(8,128)(2,1)}, bf16[2048,1408]{1,0:T(8,128)(2,1)}, bf16[1408,2048]{1,0:T(8,128)(2,1)}) custom-call(s32[12]{0:T(128)} %fusion.places, bf16[2048,2048]{1,0:T(8,128)(2,1)} %get-tuple-element.14.refs_0_, bf16[256,2048]{1,0:T(8,128)(2,1)} %get-tuple-element.15.refs_1_, ...), custom_call_target="tpu_custom_call" | custom-call | flops 11811160064 | bytes 50331648 | tf_op jit(solution)/shard_map/finish/pallas_call | solution.py:381
  150.4 0.6 collective-permute-done.end_0
  151.0 0.0 collective-permute-done.1.end_1
  151.0 1.4 place.1
Async XLA Ops:
  125.0 26.0 %collective-permute-start = (bf16[256,2048]{1,0:T(8,128)(2,1)}, bf16[256,2048]{1,0:T(8,128)(2,1)S(1)}, u32[]{:S(2)}, u32[]{:S(2)}) collective-permute-start(bf16[256,2048]{1,0:T(8,128)(2,1)} %get-tuple-element.15.refs_1_), channel_id=1, source_target_pairs={{0,1},{1,2},{2,3},{3,0},{4,5},{5,6},{6,7},{7,4},{8,9},{9,10},{10,1... | collective-permute-start | bytes 3145736 | tf_op jit(solution)/shard_map/ppermute | solution.py:430
  125.2 25.8 %collective-permute-start.1 = (bf16[256,2048]{1,0:T(8,128)(2,1)}, bf16[256,2048]{1,0:T(8,128)(2,1)S(1)}, u32[]{:S(2)}, u32[]{:S(2)}) collective-permute-start(bf16[256,2048]{1,0:T(8,128)(2,1)} %get-tuple-element.16.refs_2_), channel_id=1, source_target_pairs={{0,3},{1,0},{2,1},{3,2},{4,7},{5,4},{6,5},{7,6},{8,11},{9,8},{10,9... | collective-permute-start | bytes 3145736 | tf_op jit(solution)/shard_map/ppermute | solution.py:430

commit v2 on v1

--- a/solution.py
+++ b/solution.py
@@ -16,6 +16,7 @@
 PARTS = 2
 SUB = 4
 TILE = 256
+WIDE = 512
 
 
 def dot(a, b, dims):
@@ -24,7 +25,7 @@
 
 def ring_kernel(n, x, dy, gate, up, w_gate, w_up, w_down,
                 dx, last_0, last_1, dw_gate, dw_up, dw_down,
-                wd_v, wc_v, dy_v, g_v, u_v, ht_v, dc_v, buf, ag, x_v, xt_v, dw_v, dd_v,
+                wd_v, wc_v, dy_v, g_v, u_v, f_v, ht_v, dc_v, buf, ag, x_v, xt_v, dw_v, dd_v,
                 wd_sem, wc_sem, in_sem, send_sem, recv_sem, gsend_sem, grecv_sem, end_sem, keep_sem,
                 x_sem, dw_sem, dd_sem):
     me = lax.axis_index("tp")
@@ -54,8 +55,8 @@
         return [whole(ref.at[slot], in_sem.at[i, slot]) for i, ref in enumerate((dy_v, g_v, u_v))]
 
     def down(f):
-        rows = pl.ds(f, min(TILE, ff - f))
-        return pltpu.make_async_copy(w_down.at[rows], wd_v.at[rows], wd_sem.at[f // TILE])
+        rows = pl.ds(f, min(WIDE, ff - f))
+        return pltpu.make_async_copy(w_down.at[rows], wd_v.at[rows], wd_sem.at[f // WIDE])
 
     def weight(c):
         rows = pl.ds(pl.multiple_of(c * width, width), width)
@@ -124,47 +125,68 @@
         for copy in copies:
             copy.wait()
 
-    f_tiles = range(0, ff, TILE)
+    f_tiles = range(0, ff, WIDE)
     now, downs = load(0), [down(f) for f in f_tiles]
-    start(now[:2] + downs[:3] + now[2:] + downs[3:])
+    start(now[2:] + now[:2] + downs)
 
     barrier = pltpu.get_barrier_semaphore()
     for d in range(2):
         pl.semaphore_signal(barrier, inc=1, **to(d))
     buf[0] = jnp.zeros(buf.shape[1:], BF16)
 
-    def grads(k, first=False):
+    def span(f):
+        return pl.ds(f, min(WIDE, ff - f))
+
+    def factors(slot, cols):
+        g, u = g_v[slot, :, cols].astype(F32), u_v[slot, :, cols].astype(F32)
+        sig = jax.nn.sigmoid(g)
+        return sig * (1.0 + g * (1.0 - sig)), g * sig, u
+
+    def store_grads(k, f, d_gate, d_up):
+        for d in range(2):
+            rows, part = pl.ds(row_of(k, d), piece), slice(d * piece, (d + 1) * piece)
+            dc_v[rows, span(f)] = d_gate[part].astype(BF16)
+            dc_v[rows, pl.ds(ff + f, min(WIDE, ff - f))] = d_up[part].astype(BF16)
+
+    def store_hidden(k, f, hidden):
+        hidden = hidden.astype(BF16).T
+        for d in range(2):
+            ht_v[span(f), pl.ds(row_of(k, d), piece)] = hidden[:, d * piece:(d + 1) * piece]
+
+    def first_grads():
+        copies = loaded(0)
+        wait(copies[1:])
+        start(weight(0))
+        for f in f_tiles:
+            slope, silu, u = factors(0, span(f))
+            f_v[0, :, span(f)] = u * slope
+            f_v[1, :, span(f)] = silu
+        wait(copies[:1])
+        for f, copy in zip(f_tiles, downs):
+            copy.wait()
+            dh = dot(dy_v[0], wd_v[span(f), :], NT)
+            store_grads(0, f, dh * f_v[0, :, span(f)], dh * f_v[1, :, span(f)])
+
+    def first_hidden():
+        for f in f_tiles:
+            _, silu, u = factors(0, span(f))
+            store_hidden(0, f, silu * u)
+        start(load(2))
+
+    def grads(k):
         slot = lax.rem(k, 2)
-        copies = loaded(k)
-        wait(copies)
+        wait(loaded(k))
 
         def rest(f, dh):
-            size = min(TILE, ff - f)
-            cols = pl.ds(f, size)
-            g, u = g_v[slot, :, cols].astype(F32), u_v[slot, :, cols].astype(F32)
-            sig = jax.nn.sigmoid(g)
-            silu = g * sig
-            hidden = (silu * u).astype(BF16).T
-            d_gate = (dh * u * (sig * (1.0 + g * (1.0 - sig)))).astype(BF16)
-            d_up = (dh * silu).astype(BF16)
-            for d in range(2):
-                rows, part = pl.ds(row_of(k, d), piece), slice(d * piece, (d + 1) * piece)
-                dc_v[rows, cols] = d_gate[part]
-                dc_v[rows, pl.ds(ff + f, size)] = d_up[part]
-                ht_v[cols, rows] = hidden[:, part]
+            slope, silu, u = factors(slot, span(f))
+            store_hidden(k, f, silu * u)
+            store_grads(k, f, dh * u * slope, dh * silu)
 
         dh = None
         for f in f_tiles:
-            if first and f == 0:
-                wait(downs[:3])
-                start(weight(0))
-            if first and f == 3 * TILE:
-                rest(f - TILE, dh)
-                wait(downs[3:])
-                start(weight(1))
-            before, dh = dh, dot(dy_v[slot], wd_v[pl.ds(f, min(TILE, ff - f)), :], NT)
-            if f and not (first and f == 3 * TILE):
-                rest(f - TILE, before)
+            before, dh = dh, dot(dy_v[slot], wd_v[span(f), :], NT)
+            if f:
+                rest(f - WIDE, before)
         rest(f_tiles[-1], dh)
 
         @pl.when(k + 2 < chunks)
@@ -198,15 +220,18 @@
                 spread(0, h, c, d).start()
                 keep(0, h, c, d).start()
 
-    grads(0, first=True)
+    first_grads()
+    start(weight(1))
+    pl.semaphore_wait(barrier, 2)
+    term(0, 0, first=True)
     start(weight(2) + weight(3) + load(1))
-    pl.semaphore_wait(barrier, 2)
 
     def term0(c, _):
         term(0, c, first=True)
         return 0
 
-    lax.fori_loop(0, SUB, term0, 0)
+    lax.fori_loop(1, SUB, term0, 0)
+    first_hidden()
 
     def terms(k):
         def body(c, _):
@@ -321,6 +346,7 @@
             pltpu.VMEM((2, 2 * piece, d), BF16),
             pltpu.VMEM((2, 2 * piece, ff), BF16),
             pltpu.VMEM((2, 2 * piece, ff), BF16),
+            pltpu.VMEM((2, 2 * piece, ff), F32),
             pltpu.VMEM((ff, rows), BF16),
             pltpu.VMEM((rows, 2 * ff), BF16),
             pltpu.VMEM((n, *each, piece, width), BF16),
@@ -329,7 +355,7 @@
             pltpu.VMEM((TILE, rows), BF16),
             pltpu.VMEM((2, TILE, 2 * ff), BF16),
             pltpu.VMEM((2, ff, TILE), BF16),
-            dma((-(-ff // TILE),)),
+            dma((-(-ff // WIDE),)),
             dma((SUB,)),
             dma((3, 2)),
             dma((n - 1,)),

time: 153 us -> 152 us (level)
  no operation moved by 1% of the time
where the time goes in v2:
time: 152 us
  Pallas kernels  146 us (96%)
  starting transfers between devices  3.31 us (2%)
    pallas_call x1, Pallas kernels, ring(): pl.pallas_call(functools.partial(ring_kernel, n), out_shape=[jax.ShapeDty...  124 us
    pallas_call x1, Pallas kernels, finish(): pl.pallas_call(functools.partial(finish_kernel, count), out_shape=[jax.Sh...  21.5 us
    ppermute x2, starting transfers between devices, step(): lax.ppermute(last[d], 'tp', [(i, (i + 1 - 2 * d) % n) for i in range(n)])  3.31 us
  transfers between devices with their start and end apart: 2, of which 1 were waited for; matrix products, arithmetic and copies ran while one was open for 0% of the time, Pallas kernels for 14%

profile of v2, /device:TPU:112, one launch (start us, length us, event | category | flops | bytes accessed | tf_op | source)
XLA Modules:
  0.0 151.6 jit_solution(15739656457889489004)
XLA Ops:
  0.6 123.6 %ring.1 = (bf16[2048,2048]{1,0:T(8,128)(2,1)}, bf16[256,2048]{1,0:T(8,128)(2,1)}, bf16[256,2048]{1,0:T(8,128)(2,1)}, bf16[2048,1408]{1,0:T(8,128)(2,1)}, bf16[20...) custom-call(bf16[2048,2048]{1,0:T(8,128)(2,1)} %x.1, bf16[2048,2048]{1,0:T(8,128)(2,1)} %dy.1, bf16[2048,1408]{1,0:T(8,128)(2,1)} %gate.1, ...), custom_call_target="tpu_custom_call" | custom-call | flops 70866960384 | bytes 67108864 | tf_op jit(solution)/shard_map/ring/pallas_call | solution.py:331
  124.2 0.2 collective-permute-start
  124.4 3.1 %collective-permute-start.1 = (bf16[256,2048]{1,0:T(8,128)(2,1)}, bf16[256,2048]{1,0:T(8,128)(2,1)S(1)}, u32[]{:S(2)}, u32[]{:S(2)}) collective-permute-start(bf16[256,2048]{1,0:T(8,128)(2,1)} %get-tuple-element.16.refs_2_), channel_id=1, source_target_pairs={{0,3},{1,0},{2,1},{3,2},{4,7},{5,4},{6,5},{7,6},{8,11},{9,8},{10,9... | collective-permute-start | bytes 3145736 | tf_op jit(solution)/shard_map/ppermute | solution.py:456
  127.6 0.6 fusion.places
  128.1 21.5 %finish.1 = (bf16[2048,2048]{1,0:T(8,128)(2,1)}, bf16[2048,1408]{1,0:T(8,128)(2,1)}, bf16[2048,1408]{1,0:T(8,128)(2,1)}, bf16[1408,2048]{1,0:T(8,128)(2,1)}) custom-call(s32[12]{0:T(128)} %fusion.places, bf16[2048,2048]{1,0:T(8,128)(2,1)} %get-tuple-element.14.refs_0_, bf16[256,2048]{1,0:T(8,128)(2,1)} %get-tuple-element.15.refs_1_, ...), custom_call_target="tpu_custom_call" | custom-call | flops 11811160064 | bytes 50331648 | tf_op jit(solution)/shard_map/finish/pallas_call | solution.py:407
  149.6 0.4 collective-permute-done.end_0
  150.0 0.0 collective-permute-done.1.end_1
  150.0 1.4 place.1
Async XLA Ops:
  124.2 25.8 %collective-permute-start = (bf16[256,2048]{1,0:T(8,128)(2,1)}, bf16[256,2048]{1,0:T(8,128)(2,1)S(1)}, u32[]{:S(2)}, u32[]{:S(2)}) collective-permute-start(bf16[256,2048]{1,0:T(8,128)(2,1)} %get-tuple-element.15.refs_1_), channel_id=1, source_target_pairs={{0,1},{1,2},{2,3},{3,0},{4,5},{5,6},{6,7},{7,4},{8,9},{9,10},{10,1... | collective-permute-start | bytes 3145736 | tf_op jit(solution)/shard_map/ppermute | solution.py:456
  124.4 25.6 %collective-permute-start.1 = (bf16[256,2048]{1,0:T(8,128)(2,1)}, bf16[256,2048]{1,0:T(8,128)(2,1)S(1)}, u32[]{:S(2)}, u32[]{:S(2)}) collective-permute-start(bf16[256,2048]{1,0:T(8,128)(2,1)} %get-tuple-element.16.refs_2_), channel_id=1, source_target_pairs={{0,3},{1,0},{2,1},{3,2},{4,7},{5,4},{6,5},{7,6},{8,11},{9,8},{10,9... | collective-permute-start | bytes 3145736 | tf_op jit(solution)/shard_map/ppermute | solution.py:456

commit v3 on v2

--- a/solution.py
+++ b/solution.py
@@ -13,6 +13,7 @@
 NT = (((1,), (1,)), ((), ()))
 NN = (((1,), (0,)), ((), ()))
 TN = (((0,), (0,)), ((), ()))
+COPIES = 4
 PARTS = 2
 SUB = 4
 TILE = 256
@@ -25,7 +26,7 @@
 
 def ring_kernel(n, x, dy, gate, up, w_gate, w_up, w_down,
                 dx, last_0, last_1, dw_gate, dw_up, dw_down,
-                wd_v, wc_v, dy_v, g_v, u_v, f_v, ht_v, dc_v, buf, ag, x_v, xt_v, dw_v, dd_v,
+                wd_v, wc_v, dy_v, g_v, u_v, f_v, ht_v, dc_v, buf, ag, x_v, xt_v, dd_v,
                 wd_sem, wc_sem, in_sem, send_sem, recv_sem, gsend_sem, grecv_sem, end_sem, keep_sem,
                 x_sem, dw_sem, dd_sem):
     me = lax.axis_index("tp")
@@ -105,17 +106,12 @@
         slot = lax.rem(j, 2)
         return pltpu.make_async_copy(dd_v.at[slot], dw_down.at[:, cols], dd_sem.at[slot])
 
+    dws = (g_v, dw_gate), (u_v, dw_up)
+
     def save_dw(j):
         rows = pl.ds(pl.multiple_of(j * TILE, TILE), TILE)
         slot = lax.rem(j, 2)
-        return [
-            pltpu.make_async_copy(dw_v.at[slot, :, pl.ds(0, ff)], dw_gate.at[rows], dw_sem.at[slot]),
-            pltpu.make_async_copy(dw_v.at[slot, :, pl.ds(ff, ff)], dw_up.at[rows], dw_sem.at[slot]),
-        ]
-
-    def saved_dw(j):
-        slot = lax.rem(j, 2)
-        return whole(dw_v.at[slot], dw_sem.at[slot])
+        return [pltpu.make_async_copy(v.at[slot], out.at[rows], dw_sem.at[i, slot]) for i, (v, out) in enumerate(dws)]
 
     def start(copies):
         for copy in copies:
@@ -287,11 +283,11 @@
 
         @pl.when(j >= 2)
         def _():
-            saved_dw(j - 2).wait()
-
-        for f in range(0, 2 * ff, 2 * TILE):
-            cols = pl.ds(f, min(2 * TILE, 2 * ff - f))
-            dw_v[slot, :, cols] = dot(xt_v[...], dc_v[:, cols], NN).astype(BF16)
+            wait(save_dw(j - 2))
+
+        for i, (v, _) in enumerate(dws):
+            for f in f_tiles:
+                v[slot, :, span(f)] = dot(xt_v[...], dc_v[:, pl.ds(i * ff + f, min(WIDE, ff - f))], NN).astype(BF16)
         start(save_dw(j))
 
         @pl.when(j + 2 < tiles)
@@ -317,7 +313,7 @@
         whole(sent, gsend_sem.at[r]).wait()
     for j in range(tiles - 2, tiles):
         save_dd(j).wait()
-        saved_dw(j).wait()
+        wait(save_dw(j))
     for d, ref in enumerate((last_0, last_1)):
         whole(ref, end_sem.at[d]).wait()
 
@@ -325,7 +321,8 @@
 def ring(n, x, dy, gate, up, w_gate, w_up, w_down):
     (rows, d), ff = dy.shape, gate.shape[1]
     piece, width = rows // (2 * n * PARTS), d // SUB
-    assert n == 4 and d == PARTS * SUB * TILE
+    assert TILE == 2 * piece
+    assert n > 3 and d == PARTS * SUB * TILE
     dma = pltpu.SemaphoreType.DMA
     each = (PARTS, SUB, 2)
     return pl.pallas_call(
@@ -353,7 +350,6 @@
             pltpu.VMEM((n - 3, *each, piece, width), BF16),
             pltpu.VMEM((2, rows, TILE), BF16),
             pltpu.VMEM((TILE, rows), BF16),
-            pltpu.VMEM((2, TILE, 2 * ff), BF16),
             pltpu.VMEM((2, ff, TILE), BF16),
             dma((-(-ff // WIDE),)),
             dma((SUB,)),
@@ -365,7 +361,7 @@
             dma((2,)),
             dma((n - 2,)),
             dma((2,)),
-            dma((2,)),
+            dma((2, 2)),
             dma((2,)),
         ],
         compiler_params=pltpu.CompilerParams(
@@ -376,76 +372,76 @@
     )(x, dy, gate, up, w_gate, w_up, w_down)
 
 
-def finish_kernel(count, places, *refs):
-    del places
-    j, outs = pl.program_id(0), refs[-4:]
-    dx_in, last_0, last_1 = refs[:3]
-    for src, dst in zip(refs[3:6], outs[1:]):
-        dst[...] = src[...]
-    for low, high, src in ((0, count, dx_in), (count, count + PARTS, last_0), (count + PARTS, count + 2 * PARTS, last_1)):
-        @pl.when((j >= low) & (j < high))
-        def _():
-            outs[0][...] = src[...]
+def finish_kernel(n, dx_in, last_0, last_1, dw_gate_in, dw_up_in, dw_down_in, dx, dw_gate, dw_up, dw_down,
+                  dx_v, dg_v, du_v, dd_v, in_sem, out_sem):
+    me, half = lax.axis_index("tp"), last_0.shape[0]
+    moves = []
+    for i in range(2 * (n - 1)):
+        r, d = i // 2, i % 2
+        rows = pl.ds(pl.multiple_of((2 * lax.rem(me + (2 * d - 1) * r + n, n) + d) * half, half), half)
+        moves.append((dx_in.at[rows] if r < n - 2 else (last_0, last_1)[d], dx_v.at[i], dx.at[rows]))
+    for i in range(COPIES):
+        for src, v, dst in ((dw_gate_in, dg_v, dw_gate), (dw_up_in, du_v, dw_up), (dw_down_in, dd_v, dw_down)):
+            rows = pl.ds(i * (v.shape[0] // COPIES), v.shape[0] // COPIES)
+            moves.append((src.at[rows], v.at[rows], dst.at[rows]))
+    bring = [pltpu.make_async_copy(a, b, in_sem.at[i]) for i, (a, b, _) in enumerate(moves)]
+    put = [pltpu.make_async_copy(b, c, out_sem.at[i]) for i, (_, b, c) in enumerate(moves)]
+    for copy in bring:
+        copy.start()
+    for copy, after in zip(bring, put):
+        copy.wait()
+        after.start()
+    for copy in put:
+        copy.wait()
 
 
 def finish(n, dx, last_0, last_1, dw_gate, dw_up, dw_down):
     (rows, d), (ff, _) = dx.shape, dw_down.shape
-    piece = rows // (2 * n * PARTS)
-    count = 2 * (n - 2) * PARTS
-    me, i = lax.axis_index("tp"), jnp.arange(count + 2 * PARTS)
-    way = i // PARTS % 2
-    places = (2 * ((me + (2 * way - 1) * (i // (2 * PARTS)) + n) % n) + way) * PARTS + i % PARTS
-    steps = d // 128
-
-    def rows_in(block, most, first=0):
-        return pl.BlockSpec(block, lambda j, p: (jnp.clip(j - first, 0, most - 1), 0))
-
-    def placed(most):
-        return pl.BlockSpec((piece, d), lambda j, p: (p[jnp.minimum(j, most - 1)], 0))
-
-    weights = [rows_in((128, ff), steps), rows_in((128, ff), steps), rows_in((128, d), ff // 128)]
+    count = 2 * (n - 1) + 3 * COPIES
+    dma = pltpu.SemaphoreType.DMA
     return pl.pallas_call(
-        functools.partial(finish_kernel, count),
+        functools.partial(finish_kernel, n),
         out_shape=[jax.ShapeDtypeStruct(a.shape, a.dtype) for a in (dx, dw_gate, dw_up, dw_down)],
-        grid_spec=pltpu.PrefetchScalarGridSpec(
-            num_scalar_prefetch=1,
-            grid=(steps,),
-            in_specs=[placed(count), rows_in((piece, d), PARTS, count), rows_in((piece, d), PARTS, count + PARTS), *weights],
-            out_specs=[placed(count + 2 * PARTS), *weights],
-        ),
+        in_specs=[ANY] * 6,
+        out_specs=[ANY] * 4,
+        scratch_shapes=[
+            pltpu.VMEM((2 * (n - 1), *last_0.shape), BF16),
+            *(pltpu.VMEM(a.shape, BF16) for a in (dw_gate, dw_up, dw_down)),
+            dma((count,)),
+            dma((count,)),
+        ],
         compiler_params=pltpu.CompilerParams(vmem_limit_bytes=61 * MIB),
         cost_estimate=pl.CostEstimate(flops=2 * rows * d * ff, bytes_accessed=12 * rows * d, transcendentals=0),
         name="finish",
-    )(places, dx, last_0, last_1, dw_gate, dw_up, dw_down)
-
-
-def place_kernel(n, _, end_0, end_1, dx, sem):
-    me, half = lax.axis_index("tp"), end_0.shape[0]
-    put = []
-    for d, src in enumerate((end_0, end_1)):
-        row = (2 * lax.rem(me + (2 * d - 1) * (n - 1) + n, n) + d) * half
-        for i in range(4):
-            part = half // 4
-            rows = pl.ds(pl.multiple_of(row + i * part, part), part)
-            put.append(pltpu.make_async_copy(src.at[pl.ds(i * part, part)], dx.at[rows], sem.at[d, i]))
+    )(dx, last_0, last_1, dw_gate, dw_up, dw_down)
+
+
+def place_kernel(n, d, _, end, dx, sem):
+    me, half = lax.axis_index("tp"), end.shape[0]
+    row, part = (2 * lax.rem(me + (2 * d - 1) * (n - 1) + n, n) + d) * half, half // COPIES
+    put = [
+        pltpu.make_async_copy(
+            end.at[pl.ds(i * part, part)], dx.at[pl.ds(pl.multiple_of(row + i * part, part), part)], sem.at[i]
+        )
+        for i in range(COPIES)
+    ]
     for copy in put:
         copy.start()
     for copy in put:
         copy.wait()
 
 
-def place(n, dx, ends):
-    vmem = pl.BlockSpec(memory_space=pltpu.VMEM)
+def place(n, d, dx, end):
     return pl.pallas_call(
-        functools.partial(place_kernel, n),
+        functools.partial(place_kernel, n, d),
         out_shape=jax.ShapeDtypeStruct(dx.shape, dx.dtype),
-        in_specs=[ANY, vmem, vmem],
+        in_specs=[ANY, pl.BlockSpec(memory_space=pltpu.VMEM)],
         out_specs=ANY,
-        scratch_shapes=[pltpu.SemaphoreType.DMA((2, 4))],
+        scratch_shapes=[pltpu.SemaphoreType.DMA((COPIES,))],
         input_output_aliases={0: 0},
         compiler_params=pltpu.CompilerParams(vmem_limit_bytes=16 * MIB),
-        name="place",
-    )(dx, *ends)
+        name=f"place_{d}",
+    )(dx, end)
 
 
 def solution(mesh):
@@ -455,7 +451,9 @@
         dx, *last, dw_gate, dw_up, dw_down = ring(n, x, dy, gate, up, w_gate, w_up, w_down)
         ends = [lax.ppermute(last[d], "tp", [(i, (i + 1 - 2 * d) % n) for i in range(n)]) for d in range(2)]
         dx, dw_gate, dw_up, dw_down = finish(n, dx, *last, dw_gate, dw_up, dw_down)
-        return place(n, dx, ends), dw_gate, dw_up, dw_down
+        for d in (1, 0):
+            dx = place(n, d, dx, ends[d])
+        return dx, dw_gate, dw_up, dw_down
 
     tokens, columns, rows = P("dp", None), P(None, "tp"), P("tp", None)
     return jax.shard_map(

time: 152 us -> 152 us (level)
  waiting for transfers between devices: 0.45 us -> 5.37 us
  Pallas kernels: 146 us -> 142 us
    ppermute x2, waiting for transfers between devices: 0.45 us -> 5.37 us  [step(): lax.ppermute(last[d], 'tp', [(i, (i + 1 - 2 * d) % n) for i in range(n)])]
    pallas_call x2 -> x3, Pallas kernels: 22.8 us -> 18.3 us  [the longest x1 16.3 us: finish(): pl.pallas_call(functools.partial(finish_kernel, n), out_shape=[jax.ShapeD...]
  transfers between devices with their start and end apart: 2 -> 2, of which waited for: 1 -> 1; matrix products, arithmetic and copies ran while one was open for 0% -> 0% of each run, Pallas kernels for 14% -> 11%
where the time goes in v3:
time: 152 us; the launch traced here: 151 us
  Pallas kernels  142 us (93%)
  waiting for transfers between devices  5.37 us (4%)
  starting transfers between devices  3.31 us (2%)
    pallas_call x1, Pallas kernels, ring(): pl.pallas_call(functools.partial(ring_kernel, n), out_shape=[jax.ShapeDty...  124 us
    pallas_call x1, Pallas kernels, finish(): pl.pallas_call(functools.partial(finish_kernel, n), out_shape=[jax.ShapeD...  16.3 us
    ppermute x2, waiting for transfers between devices, step(): lax.ppermute(last[d], 'tp', [(i, (i + 1 - 2 * d) % n) for i in range(n)])  5.37 us
    ppermute x2, starting transfers between devices, step(): lax.ppermute(last[d], 'tp', [(i, (i + 1 - 2 * d) % n) for i in range(n)])  3.31 us
  transfers between devices with their start and end apart: 2, of which 1 were waited for; matrix products, arithmetic and copies ran while one was open for 0% of the time, Pallas kernels for 11%

profile of v3, /device:TPU:112, one launch (start us, length us, event | category | flops | bytes accessed | tf_op | source)
XLA Modules:
  0.0 151.5 jit_solution(3040809338761334402)
XLA Ops:
  0.6 123.6 %ring.1 = (bf16[2048,2048]{1,0:T(8,128)(2,1)}, bf16[256,2048]{1,0:T(8,128)(2,1)}, bf16[256,2048]{1,0:T(8,128)(2,1)}, bf16[2048,1408]{1,0:T(8,128)(2,1)}, bf16[20...) custom-call(bf16[2048,2048]{1,0:T(8,128)(2,1)} %x.1, bf16[2048,2048]{1,0:T(8,128)(2,1)} %dy.1, bf16[2048,1408]{1,0:T(8,128)(2,1)} %gate.1, ...), custom_call_target="tpu_custom_call" | custom-call | flops 70866960384 | bytes 67108864 | tf_op jit(solution)/shard_map/ring/pallas_call | solution.py:328
  124.3 0.2 collective-permute-start.1
  124.4 3.1 %collective-permute-start = (bf16[256,2048]{1,0:T(8,128)(2,1)}, bf16[256,2048]{1,0:T(8,128)(2,1)S(1)}, u32[]{:S(2)}, u32[]{:S(2)}) collective-permute-start(bf16[256,2048]{1,0:T(8,128)(2,1)} %get-tuple-element.16.last_1), channel_id=1, source_target_pairs={{0,3},{1,0},{2,1},{3,2},{4,7},{5,4},{6,5},{7,6},{8,11},{9,8},{10,9... | collective-permute-start | bytes 3145736 | tf_op jit(solution)/shard_map/ppermute | solution.py:452
  127.6 16.3 %finish.1 = (bf16[2048,2048]{1,0:T(8,128)(2,1)}, bf16[2048,1408]{1,0:T(8,128)(2,1)}, bf16[2048,1408]{1,0:T(8,128)(2,1)}, bf16[1408,2048]{1,0:T(8,128)(2,1)}) custom-call(bf16[2048,2048]{1,0:T(8,128)(2,1)} %get-tuple-element.14.dx_in, bf16[256,2048]{1,0:T(8,128)(2,1)} %get-tuple-element.15.last_0, bf16[256,2048]{1,0:T(8,128)(2,1)} %get-tuple-element.16.last_1, ...), custom_call_target="tpu_custom_call" | custom-call | flops 11811160064 | bytes 50331648 | tf_op jit(solution)/shard_map/finish/pallas_call | solution.py:402
  143.9 5.4 %collective-permute-done.end = bf16[256,2048]{1,0:T(8,128)(2,1)S(1)} collective-permute-done((bf16[256,2048]{1,0:T(8,128)(2,1)}, bf16[256,2048]{1,0:T(8,128)(2,1)S(1)}, u32[]{:S(2)}, u32[]{:S(2)}) %collective-permute-start) | collective-permute-done | bytes 1048608 | tf_op jit(solution)/shard_map/ppermute | solution.py:452
  149.3 1.0 place_1.1._
  150.3 0.0 collective-permute-done.1.end
  150.3 1.0 place_0.1
Async XLA Ops:
  124.3 26.0 %collective-permute-start.1 = (bf16[256,2048]{1,0:T(8,128)(2,1)}, bf16[256,2048]{1,0:T(8,128)(2,1)S(1)}, u32[]{:S(2)}, u32[]{:S(2)}) collective-permute-start(bf16[256,2048]{1,0:T(8,128)(2,1)} %get-tuple-element.15.last_0), channel_id=1, source_target_pairs={{0,1},{1,2},{2,3},{3,0},{4,5},{5,6},{6,7},{7,4},{8,9},{9,10},{10,1... | collective-permute-start | bytes 3145736 | tf_op jit(solution)/shard_map/ppermute | solution.py:452
  124.4 24.8 %collective-permute-start = (bf16[256,2048]{1,0:T(8,128)(2,1)}, bf16[256,2048]{1,0:T(8,128)(2,1)S(1)}, u32[]{:S(2)}, u32[]{:S(2)}) collective-permute-start(bf16[256,2048]{1,0:T(8,128)(2,1)} %get-tuple-element.16.last_1), channel_id=1, source_target_pairs={{0,3},{1,0},{2,1},{3,2},{4,7},{5,4},{6,5},{7,6},{8,11},{9,8},{10,9... | collective-permute-start | bytes 3145736 | tf_op jit(solution)/shard_map/ppermute | solution.py:452

commit v4 on v3

--- a/solution.py
+++ b/solution.py
@@ -75,7 +75,7 @@
     def hop(s, h, c, d):
         return pltpu.make_async_remote_copy(
             src_ref=buf.at[s, h, c, d], dst_ref=buf.at[s + 1, h, c, d],
-            send_sem=send_sem.at[s], recv_sem=recv_sem.at[s, h, c], **to(d),
+            send_sem=send_sem, recv_sem=recv_sem.at[s, h, c], **to(d),
         )
 
     def end(h, c, d):
@@ -305,8 +305,7 @@
 
     lax.fori_loop(0, tiles, tile, 0)
 
-    for s in range(n - 1):
-        whole(buf.at[s], send_sem.at[s]).wait()
+    whole(buf.at[pl.ds(0, n - 1)], send_sem).wait()
     for r in range(n - 2):
         sent = buf.at[n - 1] if r == 0 else ag.at[r - 1]
         whole(sent, keep_sem.at[r]).wait()
@@ -354,7 +353,7 @@
             dma((-(-ff // WIDE),)),
             dma((SUB,)),
             dma((3, 2)),
-            dma((n - 1,)),
+            dma(()),
             dma((n - 1, PARTS, SUB)),
             dma((n - 2,)),
             dma((n - 3, PARTS, SUB)),
@@ -421,14 +420,13 @@
     row, part = (2 * lax.rem(me + (2 * d - 1) * (n - 1) + n, n) + d) * half, half // COPIES
     put = [
         pltpu.make_async_copy(
-            end.at[pl.ds(i * part, part)], dx.at[pl.ds(pl.multiple_of(row + i * part, part), part)], sem.at[i]
+            end.at[pl.ds(i * part, part)], dx.at[pl.ds(pl.multiple_of(row + i * part, part), part)], sem
         )
         for i in range(COPIES)
     ]
     for copy in put:
         copy.start()
-    for copy in put:
-        copy.wait()
+    pltpu.make_async_copy(end, end, sem).wait()
 
 
 def place(n, d, dx, end):
@@ -437,7 +435,7 @@
         out_shape=jax.ShapeDtypeStruct(dx.shape, dx.dtype),
         in_specs=[ANY, pl.BlockSpec(memory_space=pltpu.VMEM)],
         out_specs=ANY,
-        scratch_shapes=[pltpu.SemaphoreType.DMA((COPIES,))],
+        scratch_shapes=[pltpu.SemaphoreType.DMA(())],
         input_output_aliases={0: 0},
         compiler_params=pltpu.CompilerParams(vmem_limit_bytes=16 * MIB),
         name=f"place_{d}",

time: 152 us -> 152 us (level)
  no operation moved by 1% of the time
where the time goes in v4:
time: 152 us; the launch traced here: 151 us
  Pallas kernels  142 us (93%)
  waiting for transfers between devices  5.37 us (4%)
  starting transfers between devices  3.31 us (2%)
    pallas_call x1, Pallas kernels, ring(): pl.pallas_call(functools.partial(ring_kernel, n), out_shape=[jax.ShapeDty...  124 us
    pallas_call x1, Pallas kernels, finish(): pl.pallas_call(functools.partial(finish_kernel, n), out_shape=[jax.ShapeD...  16.3 us
    ppermute x2, waiting for transfers between devices, step(): lax.ppermute(last[d], 'tp', [(i, (i + 1 - 2 * d) % n) for i in range(n)])  5.37 us
    ppermute x2, starting transfers between devices, step(): lax.ppermute(last[d], 'tp', [(i, (i + 1 - 2 * d) % n) for i in range(n)])  3.31 us
  transfers between devices with their start and end apart: 2, of which 1 were waited for; matrix products, arithmetic and copies ran while one was open for 0% of the time, Pallas kernels for 11%

profile of v4, /device:TPU:112, one launch (start us, length us, event | category | flops | bytes accessed | tf_op | source)
XLA Modules:
  0.0 151.4 jit_solution(17418967247865860589)
XLA Ops:
  0.6 123.6 %ring.1 = (bf16[2048,2048]{1,0:T(8,128)(2,1)}, bf16[256,2048]{1,0:T(8,128)(2,1)}, bf16[256,2048]{1,0:T(8,128)(2,1)}, bf16[2048,1408]{1,0:T(8,128)(2,1)}, bf16[20...) custom-call(bf16[2048,2048]{1,0:T(8,128)(2,1)} %x.1, bf16[2048,2048]{1,0:T(8,128)(2,1)} %dy.1, bf16[2048,1408]{1,0:T(8,128)(2,1)} %gate.1, ...), custom_call_target="tpu_custom_call" | custom-call | flops 70866960384 | bytes 67108864 | tf_op jit(solution)/shard_map/ring/pallas_call | solution.py:327
  124.2 0.2 collective-permute-start.1
  124.4 3.1 %collective-permute-start = (bf16[256,2048]{1,0:T(8,128)(2,1)}, bf16[256,2048]{1,0:T(8,128)(2,1)S(1)}, u32[]{:S(2)}, u32[]{:S(2)}) collective-permute-start(bf16[256,2048]{1,0:T(8,128)(2,1)} %get-tuple-element.16.last_1), channel_id=1, source_target_pairs={{0,3},{1,0},{2,1},{3,2},{4,7},{5,4},{6,5},{7,6},{8,11},{9,8},{10,9... | collective-permute-start | bytes 3145736 | tf_op jit(solution)/shard_map/ppermute | solution.py:450
  127.6 16.3 %finish.1 = (bf16[2048,2048]{1,0:T(8,128)(2,1)}, bf16[2048,1408]{1,0:T(8,128)(2,1)}, bf16[2048,1408]{1,0:T(8,128)(2,1)}, bf16[1408,2048]{1,0:T(8,128)(2,1)}) custom-call(bf16[2048,2048]{1,0:T(8,128)(2,1)} %get-tuple-element.14.dx_in, bf16[256,2048]{1,0:T(8,128)(2,1)} %get-tuple-element.15.last_0, bf16[256,2048]{1,0:T(8,128)(2,1)} %get-tuple-element.16.last_1, ...), custom_call_target="tpu_custom_call" | custom-call | flops 11811160064 | bytes 50331648 | tf_op jit(solution)/shard_map/finish/pallas_call | solution.py:401
  143.9 5.4 %collective-permute-done.end = bf16[256,2048]{1,0:T(8,128)(2,1)S(1)} collective-permute-done((bf16[256,2048]{1,0:T(8,128)(2,1)}, bf16[256,2048]{1,0:T(8,128)(2,1)S(1)}, u32[]{:S(2)}, u32[]{:S(2)}) %collective-permute-start) | collective-permute-done | bytes 1048608 | tf_op jit(solution)/shard_map/ppermute | solution.py:450
  149.3 1.0 place_1.1._
  150.2 0.0 collective-permute-done.1.end
  150.3 1.0 place_0.1
Async XLA Ops:
  124.2 26.0 %collective-permute-start.1 = (bf16[256,2048]{1,0:T(8,128)(2,1)}, bf16[256,2048]{1,0:T(8,128)(2,1)S(1)}, u32[]{:S(2)}, u32[]{:S(2)}) collective-permute-start(bf16[256,2048]{1,0:T(8,128)(2,1)} %get-tuple-element.15.last_0), channel_id=1, source_target_pairs={{0,1},{1,2},{2,3},{3,0},{4,5},{5,6},{6,7},{7,4},{8,9},{9,10},{10,1... | collective-permute-start | bytes 3145736 | tf_op jit(solution)/shard_map/ppermute | solution.py:450
  124.4 24.8 %collective-permute-start = (bf16[256,2048]{1,0:T(8,128)(2,1)}, bf16[256,2048]{1,0:T(8,128)(2,1)S(1)}, u32[]{:S(2)}, u32[]{:S(2)}) collective-permute-start(bf16[256,2048]{1,0:T(8,128)(2,1)} %get-tuple-element.16.last_1), channel_id=1, source_target_pairs={{0,3},{1,0},{2,1},{3,2},{4,7},{5,4},{6,5},{7,6},{8,11},{9,8},{10,9... | collective-permute-start | bytes 3145736 | tf_op jit(solution)/shard_map/ppermute | solution.py:450
